TPU v7x, 128 devices: a whole 4x4x4 slice. The times are simulated.
128 devices in a mesh: wide: 32 (over y, z, core), narrow: 4 (over x).
Axes of the slice: x: 4, y: 4, z: 4, core: 2. Of those that a mesh axis runs over, the one named last changes fastest.
Arguments:
- object_field: float32 [2, 2048, 16384], P(None, 'narrow', 'wide')
- probe: float32 [4, 2, 256, 256], replicated, may hold values from -3 to 3
- patterns: float32 [4, 32, 6, 256, 256], P('narrow', 'wide'), may hold values from 0.1 to 4
- offsets: int32 [4, 32, 6, 2], P('narrow', 'wide'), may hold values from -128 to 384
- counts: int32 [4, 32], P('narrow', 'wide'), may hold values from 1 to 6
Outputs:
- object_new: float32 [2, 2048, 16384], P(None, 'narrow', 'wide')
- probe_new: float32 [4, 2, 256, 256], replicated
Inputs may be any that keep to these rules, and one draw needn't show every extreme that they name: A patch of 256 x 256 pixels at these offsets stays within the tile extended by 128 pixels on each side. `counts`: slots 0 to count - 1 of a tile are live, the others are ignored.
All inputs are finite; a program needn't handle non-finite values.
Results may differ from a plain program's by a relative error of at most 0.0003.
Values sent between devices are 32-bit elements; how exact they have to be, the bound alone decides.
A program may use at most 128 MiB of HBM per device.

v0:
```python
import jax
import jax.numpy as jnp
from jax import lax
from jax.sharding import PartitionSpec as P

H = 128
BATCHES = 3
POS = 2


def extended(shard, sides, width):
    for axis, dim in sides:
        size, length = (lax.axis_size(axis), shard.shape[dim])
        up = [(i, (i + 1) % size) for i in range(size - 1)]
        down = [(j, i) for i, j in up]
        last = lax.slice_in_dim(shard, length - width, length, axis=dim)
        leading = lax.slice_in_dim(shard, 0, width, axis=dim)
        before = lax.ppermute(last, axis, up)
        after = lax.ppermute(leading, axis, down)
        shard = jnp.concatenate([before, shard, after], axis=dim)
    return shard


def shifted(value, axis, steps):
    count = lax.axis_size(axis)
    leading, last = (max(0, -steps), min(count, count - steps))
    return lax.ppermute(value, axis, [(source, source + steps) for source in range(leading, last)])


def dft_tables(size):
    index = jnp.arange(size, dtype=jnp.int32)
    phase = index[:, None] * index[None, :] % size
    angle = -2.0 * jnp.pi * phase.astype(jnp.float32) / size
    scale = 1.0 / jnp.sqrt(jnp.float32(size))
    return (jnp.cos(angle) * scale, jnp.sin(angle) * scale)


def transform(real_part, imag_part, table_re, table_im):
    high = lax.Precision.HIGHEST
    left_re = jnp.einsum("jk,mkl->mjl", table_re, real_part, precision=high) - jnp.einsum(
        "jk,mkl->mjl", table_im, imag_part, precision=high
    )
    left_im = jnp.einsum("jk,mkl->mjl", table_re, imag_part, precision=high) + jnp.einsum(
        "jk,mkl->mjl", table_im, real_part, precision=high
    )
    out_re = jnp.einsum("mjk,kl->mjl", left_re, table_re, precision=high) - jnp.einsum(
        "mjk,kl->mjl", left_im, table_im, precision=high
    )
    out_im = jnp.einsum("mjk,kl->mjl", left_re, table_im, precision=high) + jnp.einsum(
        "mjk,kl->mjl", left_im, table_re, precision=high
    )
    return (out_re, out_im)


def slot_terms(patch, probe, measured, table_re, table_im):
    probe_re = probe[:, 0]
    probe_im = probe[:, 1]
    obj_re = patch[0]
    obj_im = patch[1]
    psi_re = probe_re * obj_re - probe_im * obj_im
    psi_im = probe_re * obj_im + probe_im * obj_re
    far_re, far_im = transform(psi_re, psi_im, table_re, table_im)
    intensity = jnp.sum(far_re * far_re + far_im * far_im, axis=0)
    keep = 1.0 - jnp.sqrt(measured) / jnp.sqrt(intensity + 0.1)
    back_re, back_im = transform(far_re * keep, far_im * keep, table_re, -table_im)
    grad_re = jnp.sum(probe_re * back_re + probe_im * back_im, axis=0)
    grad_im = jnp.sum(probe_re * back_im - probe_im * back_re, axis=0)
    pgrad_re = obj_re * back_re + obj_im * back_im
    pgrad_im = obj_re * back_im - obj_im * back_re
    square = jnp.sum(obj_re * obj_re + obj_im * obj_im)
    return (jnp.stack([grad_re, grad_im]), jnp.stack([pgrad_re, pgrad_im], axis=1), square)


def local(object_field, probe, patterns, offsets, counts):
    tile = object_field.shape[1]
    size = probe.shape[-1]
    table_re, table_im = dft_tables(size)
    padded = extended(object_field, (("wide", 2), ("narrow", 1)), H)
    gradient = jnp.zeros_like(padded)
    count_here = counts[0, 0]
    zero_at = jnp.zeros((), jnp.int32)
    for minibatch in range(BATCHES):
        probe_grad = jnp.zeros_like(probe)
        coverage = jnp.zeros((), jnp.float32)
        for position in range(POS):
            slot_at = minibatch * POS + position
            row_at = offsets[0, 0, slot_at, 0] + H
            col_at = offsets[0, 0, slot_at, 1] + H
            patch = lax.dynamic_slice(padded, (zero_at, row_at, col_at), (2, size, size))
            measured = patterns[0, 0, slot_at]

            def active(operands):
                return slot_terms(operands[0], operands[1], operands[2], table_re, table_im)

            def inactive(operands):
                return (
                    jnp.zeros((2, size, size), jnp.float32),
                    jnp.zeros_like(probe),
                    jnp.zeros((), jnp.float32),
                )

            obj_grad, pgrad, square = lax.cond(
                slot_at < count_here, active, inactive, (patch, probe, measured)
            )
            old = lax.dynamic_slice(gradient, (zero_at, row_at, col_at), (2, size, size))
            gradient = lax.dynamic_update_slice(gradient, old + obj_grad, (zero_at, row_at, col_at))
            probe_grad = probe_grad + pgrad
            coverage = coverage + square
        summed, total_cover = lax.psum((probe_grad, coverage), ("wide", "narrow"))
        probe = probe - summed / (total_cover / (size * size))
    left_part = gradient[:, :, :H]
    right_part = gradient[:, :, tile + H :]
    from_right = shifted(left_part, "wide", -1)
    from_left = shifted(right_part, "wide", 1)
    gradient = gradient.at[:, :, tile : tile + H].add(from_right)
    gradient = gradient.at[:, :, H : 2 * H].add(from_left)
    upper_part = gradient[:, :H, H : tile + H]
    lower_part = gradient[:, tile + H :, H : tile + H]
    from_below = shifted(upper_part, "narrow", -1)
    from_above = shifted(lower_part, "narrow", 1)
    core = gradient[:, H : tile + H, H : tile + H]
    core = core.at[:, tile - H :, :].add(from_below)
    core = core.at[:, :H, :].add(from_above)
    power = jnp.sum(probe[:, 0] ** 2 + probe[:, 1] ** 2, axis=0)
    top = jnp.max(power)
    return (object_field - 0.5 * core / top, probe)


def solution(mesh):
    placed = (
        P(None, "narrow", "wide"),
        P(),
        P("narrow", "wide", None, None, None),
        P("narrow", "wide", None, None),
        P("narrow", "wide"),
    )
    return jax.shard_map(
        local,
        mesh=mesh,
        in_specs=placed,
        out_specs=(P(None, "narrow", "wide"), P()),
        check_vma=False,
    )
```

profile of v0, /device:TPU:1, one launch (start us, length us, event | category | flops | bytes accessed | tf_op | source)
XLA Modules:
  0.0 804.1 jit_solution(2545430750540542145)
XLA Ops:
  8.6 4.9 collective-permute-start
  13.6 1.9 collective-permute-start.1
  15.5 4.2 collective-permute-done
  19.9 4.2 collective-permute-done.1
  27.1 3.2 collective-permute-start.2
  38.9 2.7 collective-permute-done.2
  41.6 4.1 collective-permute-done.3
  45.7 4.6 pad_maximum_fusion.12
  50.3 37.6 %conditional.6 = (f32[2,256,256]{2,1,0:T(8,128)S(1)}, f32[]{:T(128)}, f32[4,2,256,256]{3,2,1,0:T(8,128)}) conditional(s32[]{:T(128)} %bitcast.174, () %tuple.80, (f32[4,2,256,256]{3,2,1,0:T(8,128)S(1)}, f32[2,768,768]{2,1,0:T(8,128)}, f32[256,256]{1,0:T(8,128)S(1)}, f32[256,256]{1,0:T(8,128)S(1)}, f32[256,256]{1,0:T(8,128)S(1)}, ...), branch_computations={%region_0.1_spmd, %region_1.6_spmd.clone} | conditional | flops 12897091584 | bytes 71303224 | solution.py:102
  50.8 2.0 add_reduce_fusion.14
  60.3 1.9 fusion.189
  62.1 1.9 fusion.196
  64.0 2.0 convolution_subtract_fusion.18
  66.1 2.0 add_reduce_fusion.13
  78.2 2.0 fusion.184
  80.2 1.9 convolution_add_fusion.16
  82.1 2.4 add_bitcast_fusion.4
  87.9 38.3 %conditional.7 = (f32[2,256,256]{2,1,0:T(8,128)S(1)}, f32[]{:T(128)}, f32[4,2,256,256]{3,2,1,0:T(8,128)}) conditional(s32[]{:T(128)} %bitcast.183, () %tuple.82, (f32[4,2,256,256]{3,2,1,0:T(8,128)S(1)}, f32[2,768,768]{2,1,0:T(8,128)}, f32[256,256]{1,0:T(8,128)S(1)}, f32[256,256]{1,0:T(8,128)S(1)}, f32[256,256]{1,0:T(8,128)S(1)}, ...), branch_computations={%region_6.7_spmd, %region_7.12_spmd.clone} | conditional | flops 12897091584 | bytes 71303224 | solution.py:102
  88.0 1.9 add_reduce_fusion.17
  91.8 1.9 fusion.207
  97.4 1.9 fusion.230
  99.2 1.9 fusion.237
  101.1 2.0 convolution_subtract_fusion.22
  103.2 2.0 add_reduce_fusion.16
  115.3 2.0 fusion.225
  117.4 1.9 convolution_add_fusion.20
  119.2 2.4 add_bitcast_fusion.5
  126.2 4.0 add.745
  135.5 71.5 %psum.43 = f32[]{:T(128)} all-reduce(f32[]{:T(128)S(6)} %add.746), channel_id=1, replica_groups=mesh['wide'=32,'narrow'=4] {'wide','narrow'}, use_global_device_ids=true, to_apply=%region_13.14 | all-reduce | flops 1 | bytes 8 | tf_op jit(solution)/shard_map/psum | solution.py:109
  207.7 80.3 %all-reduce.4.cloned.1.call-done = f32[4,2,256,256]{3,2,1,0:T(8,128)} async-done(((f32[4,2,256,256]{3,2,1,0:T(8,128)}), f32[4,2,256,256]{3,2,1,0:T(8,128)}) %all-reduce.4.cloned.1.call-update) | async-done | bytes 2097168 | tf_op jit(solution)/shard_map/psum | solution.py:109
  288.1 2.6 divide_subtract_fusion.3
  290.6 37.3 %conditional.8 = (f32[2,256,256]{2,1,0:T(8,128)}, f32[]{:T(128)}, f32[4,2,256,256]{3,2,1,0:T(8,128)}) conditional(s32[]{:T(128)} %bitcast.188, () %tuple.84, (f32[4,2,256,256]{3,2,1,0:T(8,128)S(1)}, f32[2,768,768]{2,1,0:T(8,128)}, s32[]{:T(128)}, s32[]{:T(128)}, f32[256,256]{1,0:T(8,128)S(1)}, /*index=5*/f32[256,256]{1,0:T(8,128)S(1)}, ...), branch_computations={%region_14.15_spmd, %region_15.20_spmd} | conditional | flops 12897091584 | bytes 71303224 | solution.py:102
  290.7 2.0 add_reduce_fusion.2
  300.1 1.9 fusion.25
  302.0 1.9 fusion.32
  303.9 2.0 convolution_subtract_fusion.2
  305.9 2.0 add_reduce_fusion.1
  318.1 2.0 fusion.20
  320.1 1.9 convolution_add_fusion
  322.0 2.4 add_bitcast_fusion
  327.9 12.4 %conditional.9 = (f32[2,256,256]{2,1,0:T(8,128)}, f32[]{:T(128)}, f32[4,2,256,256]{3,2,1,0:T(8,128)}) conditional(s32[]{:T(128)} %bitcast.193, () %tuple.86, (f32[4,2,256,256]{3,2,1,0:T(8,128)S(1)}, f32[2,768,768]{2,1,0:T(8,128)}, s32[]{:T(128)}, s32[]{:T(128)}, f32[256,256]{1,0:T(8,128)S(1)}, /*index=5*/f32[256,256]{1,0:T(8,128)S(1)}, ...), branch_computations={%region_20.21_spmd, %region_21.26_spmd} | conditional | flops 12897091584 | bytes 71303224 | solution.py:102
  340.3 3.8 add.765
  348.9 2.5 broadcast_in_dim.2
  351.4 6.5 dynamic_update_slice.18
  359.4 6.6 dynamic_update_slice.19
  366.1 89.8 %psum.45 = f32[]{:T(128)} all-reduce(f32[]{:T(128)S(6)} %add.766), channel_id=1, replica_groups=mesh['wide'=32,'narrow'=4] {'wide','narrow'}, use_global_device_ids=true, to_apply=%region_27.28 | all-reduce | flops 1 | bytes 8 | tf_op jit(solution)/shard_map/psum | solution.py:109
  458.1 6.4 dynamic_update_slice.20
  466.0 6.6 dynamic_update_slice.21
  472.6 45.5 %all-reduce.6.cloned.1.call-done = f32[4,2,256,256]{3,2,1,0:T(8,128)} async-done(((f32[4,2,256,256]{3,2,1,0:T(8,128)}), f32[4,2,256,256]{3,2,1,0:T(8,128)}) %all-reduce.6.cloned.1.call-update) | async-done | bytes 2097168 | tf_op jit(solution)/shard_map/psum | solution.py:109
  518.1 3.2 divide_subtract_fusion.2
  521.3 11.7 %conditional.10 = (f32[2,256,256]{2,1,0:T(8,128)}, f32[]{:T(128)}, f32[4,2,256,256]{3,2,1,0:T(8,128)}) conditional(s32[]{:T(128)} %bitcast.198, () %tuple.88, (f32[4,2,256,256]{3,2,1,0:T(8,128)}, f32[2,768,768]{2,1,0:T(8,128)}, s32[]{:T(128)}, s32[]{:T(128)}, f32[256,256]{1,0:T(8,128)S(1)}, /*index=5*/f32[256,256]{1,0:T(8,128)S(1)}, ...), branch_computations={%region_28.29_spmd, %region_29.34_spmd} | conditional | flops 12897091584 | bytes 79691856 | solution.py:102
  534.6 6.8 dynamic_update_slice.22
  541.4 5.4 conditional.11
  548.2 6.9 dynamic_update_slice.23
  556.3 60.8 %collective-permute-start.4 = (f32[2,768,128]{2,1,0:T(8,128)S(1)}, f32[2,768,128]{2,1,0:T(8,128)S(1)}, u32[]{:S(2)}, u32[]{:S(2)}) collective-permute-start(f32[2,768,128]{2,1,0:T(8,128)S(1)} %slice.336), channel_id=1, source_target_pairs={{4,0},{8,4},{12,8},{16,12},{20,16},{24,20},{28,24},{32,28},{36,32}... | collective-permute-start | bytes 2359304 | tf_op jit(solution)/shard_map/ppermute | solution.py:27
  617.1 1.9 collective-permute-done.4
  619.0 2.7 fusion.259
  621.8 1.9 collective-permute-start.5
  623.7 3.8 add.781
  627.5 75.8 %psum.47 = f32[]{:T(128)} all-reduce(f32[]{:T(128)S(6)} %add.782), channel_id=1, replica_groups=mesh['wide'=32,'narrow'=4] {'wide','narrow'}, use_global_device_ids=true, to_apply=%region_41.42 | all-reduce | flops 1 | bytes 8 | tf_op jit(solution)/shard_map/psum | solution.py:109
  703.9 2.2 fusion.248
  706.1 2.3 fusion.258
  711.0 76.2 %all-reduce.8.cloned.1.call-done = f32[4,2,256,256]{3,2,1,0:T(8,128)} async-done(((f32[4,2,256,256]{3,2,1,0:T(8,128)}), f32[4,2,256,256]{3,2,1,0:T(8,128)}) %all-reduce.8.cloned.1.call-update) | async-done | bytes 2097168 | tf_op jit(solution)/shard_map/psum | solution.py:109
  794.9 2.4 divide_subtract_fusion
  (91 shorter events, 89.7 us)
Async XLA Ops:
  7.2 12.6 %copy-start.3 = (f32[2,512,512]{2,1,0:T(8,128)S(1)}, f32[2,512,512]{2,1,0:T(8,128)}, u32[]{:S(2)}) copy-start(f32[2,512,512]{2,1,0:T(8,128)} %param.25) | copy-start | bytes 6291460
  7.2 280.9 %all-reduce.4.cloned.1.call-start = ((), (), s32[]{:S(2)}) async-start(), calls=%async_computation | async-start | bytes 4194304 | tf_op jit(solution)/shard_map/psum | solution.py:109
  8.6 11.0 %collective-permute-start = (f32[2,512,128]{2,1,0:T(8,128)S(1)}, f32[2,512,128]{2,1,0:T(8,128)S(1)}, u32[]{:S(2)}, u32[]{:S(2)}) collective-permute-start(f32[2,512,128]{2,1,0:T(8,128)S(1)} %get-tuple-element.871), channel_id=1, source_target_pairs={{0,4},{4,8},{8,12},{12,16},{16,20},{20,24},{24,28},{28,32},{32,36}... | collective-permute-start | bytes 1572872 | tf_op jit(solution)/shard_map/ppermute | solution.py:18
  13.6 10.5 %collective-permute-start.1 = (f32[2,512,128]{2,1,0:T(8,128)S(1)}, f32[2,512,128]{2,1,0:T(8,128)S(1)}, u32[]{:S(2)}, u32[]{:S(2)}) collective-permute-start(f32[2,512,128]{2,1,0:T(8,128)S(1)} %get-tuple-element.870), channel_id=1, source_target_pairs={{4,0},{8,4},{12,8},{16,12},{20,16},{24,20},{28,24},{32,28},{36,32}... | collective-permute-start | bytes 1572872 | tf_op jit(solution)/shard_map/ppermute | solution.py:19
  19.9 11.6 %copy-start.8 = (s32[1,1,6,2]{2,3,1,0:T(2,128)S(1)}, s32[1,1,6,2]{2,3,1,0:T(2,128)}, u32[]{:S(2)}) copy-start(s32[1,1,6,2]{2,3,1,0:T(2,128)} %param.28) | copy-start | bytes 148
  24.1 1.7 copy-start.5
  27.1 14.5 %collective-permute-start.2 = (f32[2,128,768]{2,1,0:T(8,128)}, f32[2,128,768]{2,1,0:T(8,128)S(1)}, u32[]{:S(2)}, u32[]{:S(2)}) collective-permute-start(f32[2,128,768]{2,1,0:T(8,128)} %get-tuple-element.868), channel_id=1, source_target_pairs={{0,1},{1,2},{2,3},{4,5},{5,6},{6,7},{8,9},{9,10},{10,11},{12,13},{... | collective-permute-start | bytes 2359304 | tf_op jit(solution)/shard_map/ppermute | solution.py:18
  30.2 15.5 %collective-permute-start.3 = (f32[2,128,768]{2,1,0:T(8,128)}, f32[2,128,768]{2,1,0:T(8,128)}, u32[]{:S(2)}, u32[]{:S(2)}) collective-permute-start(f32[2,128,768]{2,1,0:T(8,128)} %get-tuple-element.869), channel_id=1, source_target_pairs={{1,0},{2,1},{3,2},{5,4},{6,5},{7,6},{9,8},{10,9},{11,10},{13,12},{... | collective-permute-start | bytes 2359304 | tf_op jit(solution)/shard_map/ppermute | solution.py:19
  38.9 11.4 %copy-start.2 = (f32[4,2,256,256]{3,2,1,0:T(8,128)S(1)}, f32[4,2,256,256]{3,2,1,0:T(8,128)}, u32[]{:S(2)}) copy-start(f32[4,2,256,256]{3,2,1,0:T(8,128)} %param.26) | copy-start | bytes 6291460
  126.2 4.0 copy-start.7
  130.3 387.8 %all-reduce.6.cloned.1.call-start = ((), (), s32[]{:S(2)}) async-start(), calls=%async_computation.1 | async-start | bytes 4194304 | tf_op jit(solution)/shard_map/psum | solution.py:109
  344.1 443.1 %all-reduce.8.cloned.1.call-start = ((), (), s32[]{:S(2)}) async-start(), calls=%async_computation.2 | async-start | bytes 4194304 | tf_op jit(solution)/shard_map/psum | solution.py:109
  532.9 8.5 %copy-start = (f32[4,2,256,256]{3,2,1,0:T(8,128)S(1)}, f32[4,2,256,256]{3,2,1,0:T(8,128)}, u32[]{:S(2)}) copy-start(f32[4,2,256,256]{3,2,1,0:T(8,128)} %divide_subtract_fusion.2) | copy-start | bytes 6291460
  556.3 62.7 %collective-permute-start.4 = (f32[2,768,128]{2,1,0:T(8,128)S(1)}, f32[2,768,128]{2,1,0:T(8,128)S(1)}, u32[]{:S(2)}, u32[]{:S(2)}) collective-permute-start(f32[2,768,128]{2,1,0:T(8,128)S(1)} %slice.336), channel_id=1, source_target_pairs={{4,0},{8,4},{12,8},{16,12},{20,16},{24,20},{28,24},{32,28},{36,32}... | collective-permute-start | bytes 2359304 | tf_op jit(solution)/shard_map/ppermute | solution.py:27
  621.8 82.2 %collective-permute-start.5 = (f32[2,768,128]{2,1,0:T(8,128)}, f32[2,768,128]{2,1,0:T(8,128)S(1)}, u32[]{:S(2)}, u32[]{:S(2)}) collective-permute-start(f32[2,768,128]{2,1,0:T(8,128)} %get-tuple-element.866), channel_id=1, source_target_pairs={{0,4},{4,8},{8,12},{12,16},{16,20},{20,24},{24,28},{28,32},{32,36}... | collective-permute-start | bytes 2359304 | tf_op jit(solution)/shard_map/ppermute | solution.py:27
  708.4 86.1 %collective-permute-start.7 = (f32[2,128,512]{2,1,0:T(8,128)}, f32[2,128,512]{2,1,0:T(8,128)S(1)}, u32[]{:S(2)}, u32[]{:S(2)}) collective-permute-start(f32[2,128,512]{2,1,0:T(8,128)} %get-tuple-element.864), channel_id=1, source_target_pairs={{0,1},{1,2},{2,3},{4,5},{5,6},{6,7},{8,9},{9,10},{10,11},{12,13},{... | collective-permute-start | bytes 1572872 | tf_op jit(solution)/shard_map/ppermute | solution.py:27
  709.7 83.3 %collective-permute-start.6 = (f32[2,128,512]{2,1,0:T(8,128)}, f32[2,128,512]{2,1,0:T(8,128)}, u32[]{:S(2)}, u32[]{:S(2)}) collective-permute-start(f32[2,128,512]{2,1,0:T(8,128)} %get-tuple-element.865), channel_id=1, source_target_pairs={{1,0},{2,1},{3,2},{5,4},{6,5},{7,6},{9,8},{10,9},{11,10},{13,12},{... | collective-permute-start | bytes 1572872 | tf_op jit(solution)/shard_map/ppermute | solution.py:27
  789.1 1.3 copy-start.6
  793.0 1.9 copy-start.4
Sparse Core Ops, SparseCore 0:
  130.4 157.6 all-reduce.3
  344.3 173.7 all-reduce.5
  627.6 159.5 all-reduce.7
where the time goes:
time: 809 us; the launch traced here: 804 us
  blocking collectives  237 us (29%)
  waiting for transfers between devices  219 us (27%)
  matrix products  91.7 us (11%)
  starting transfers between devices  76.8 us (9%)
  local copies, waits for them, and re-layouts  65 us (8%)
  other arithmetic  52.5 us (6%)
  between operations  31.9 us (4%)
  loops' own time  29.9 us (4%)
    psum x3, blocking collectives, local(): summed, total_cover = lax.psum((probe_grad, coverage), ('wide', 'narrow'))  237 us
    psum x3, waiting for transfers between devices, local(): summed, total_cover = lax.psum((probe_grad, coverage), ('wide', 'narrow'))  202 us
    ppermute x4, starting transfers between devices, shifted(): lax.ppermute(value, axis, [(source, source + steps) for source in range(l...  65.4 us
    dynamic_update_slice x6, local copies, waits for them, and re-layouts, local(): lax.dynamic_update_slice(gradient, old + obj_grad, (zero_at, row_at, col_...  39.8 us
    another operation x6, loops' own time, local(): lax.cond(slot_at < count_here, active, inactive, (patch, probe, measured))  29.9 us
  transfers between devices with their start and end apart: 11, of which 8 were waited for; matrix products, arithmetic and copies ran while one was open for 6% of the time, Pallas kernels for 0%

commit v1 on v0

--- a/solution.py
+++ b/solution.py
@@ -106,7 +106,7 @@
             gradient = lax.dynamic_update_slice(gradient, old + obj_grad, (zero_at, row_at, col_at))
             probe_grad = probe_grad + pgrad
             coverage = coverage + square
-        summed, total_cover = lax.psum((probe_grad, coverage), ("wide", "narrow"))
+        summed, total_cover = lax.psum(lax.psum((probe_grad, coverage), "wide"), "narrow")
         probe = probe - summed / (total_cover / (size * size))
     left_part = gradient[:, :, :H]
     right_part = gradient[:, :, tile + H :]

time: 809 us -> 945 us (1.17)
  waiting for transfers between devices: 219 us -> 359 us
  blocking collectives: 237 us -> 216 us
    psum x3 -> x6, waiting for transfers between devices: 202 us -> 343 us  [the longest x3 343 us: local(): lax.psum((probe_grad, coverage), 'wide')]
    psum x3 -> x6, blocking collectives: 237 us -> 216 us  [the longest x3 190 us: local(): lax.psum((probe_grad, coverage), 'wide')]
  transfers between devices with their start and end apart: 11 -> 14, of which waited for: 8 -> 7; matrix products, arithmetic and copies ran while one was open for 6% -> 6% of each run, Pallas kernels for 0% -> 0%
where the time goes in v1:
time: 945 us; the launch traced here: 935 us
  waiting for transfers between devices  359 us (38%)
  blocking collectives  216 us (23%)
  matrix products  91.7 us (10%)
  starting transfers between devices  85.4 us (9%)
  local copies, waits for them, and re-layouts  66.7 us (7%)
  other arithmetic  57.5 us (6%)
  between operations  32 us (3%)
  loops' own time  27.3 us (3%)
    psum x3, waiting for transfers between devices, local(): lax.psum((probe_grad, coverage), 'wide')  343 us
    psum x3, blocking collectives, local(): lax.psum((probe_grad, coverage), 'wide')  190 us
    ppermute x4, starting transfers between devices, shifted(): lax.ppermute(value, axis, [(source, source + steps) for source in range(l...  73.9 us
    dynamic_update_slice x6, local copies, waits for them, and re-layouts, local(): lax.dynamic_update_slice(gradient, old + obj_grad, (zero_at, row_at, col_...  39.8 us
    another operation x6, loops' own time, local(): lax.cond(slot_at < count_here, active, inactive, (patch, probe, measured))  27.3 us
    psum x3, blocking collectives, local(): lax.psum(lax.psum((probe_grad, coverage), 'wide'), 'narrow')  26.1 us
  transfers between devices with their start and end apart: 14, of which 7 were waited for; matrix products, arithmetic and copies ran while one was open for 6% of the time, Pallas kernels for 0%

profile of v1, /device:TPU:1, one launch (start us, length us, event | category | flops | bytes accessed | tf_op | source)
XLA Modules:
  0.0 935.2 jit_solution(13289251375042594683)
XLA Ops:
  8.6 4.9 collective-permute-start
  13.6 1.9 collective-permute-start.1
  15.5 4.2 collective-permute-done
  19.9 4.2 collective-permute-done.1
  27.1 3.2 collective-permute-start.2
  38.8 2.8 collective-permute-done.2
  41.6 4.1 collective-permute-done.3
  45.7 4.6 pad_maximum_fusion.12
  50.3 37.7 %conditional.6 = (f32[2,256,256]{2,1,0:T(8,128)S(1)}, f32[]{:T(128)}, f32[4,2,256,256]{3,2,1,0:T(8,128)}) conditional(s32[]{:T(128)} %bitcast.174, () %tuple.80, (f32[4,2,256,256]{3,2,1,0:T(8,128)S(1)}, f32[2,768,768]{2,1,0:T(8,128)}, f32[256,256]{1,0:T(8,128)S(1)}, f32[256,256]{1,0:T(8,128)S(1)}, f32[256,256]{1,0:T(8,128)S(1)}, ...), branch_computations={%region_0.1_spmd, %region_1.6_spmd.clone} | conditional | flops 12897091584 | bytes 71303224 | solution.py:102
  50.8 2.0 add_reduce_fusion.14
  62.2 1.9 fusion.196
  64.1 2.0 convolution_subtract_fusion.18
  66.1 2.0 add_reduce_fusion.13
  78.3 2.0 fusion.184
  80.3 1.9 convolution_add_fusion.16
  82.2 2.4 add_bitcast_fusion.4
  88.0 37.8 %conditional.7 = (f32[2,256,256]{2,1,0:T(8,128)}, f32[]{:T(128)}, f32[4,2,256,256]{3,2,1,0:T(8,128)}) conditional(s32[]{:T(128)} %bitcast.183, () %tuple.82, (f32[4,2,256,256]{3,2,1,0:T(8,128)S(1)}, f32[2,768,768]{2,1,0:T(8,128)}, f32[256,256]{1,0:T(8,128)S(1)}, f32[256,256]{1,0:T(8,128)S(1)}, f32[256,256]{1,0:T(8,128)S(1)}, ...), branch_computations={%region_6.7_spmd, %region_7.12_spmd.clone} | conditional | flops 12897091584 | bytes 71303224 | solution.py:102
  88.0 2.0 add_reduce_fusion.17
  101.2 2.0 convolution_subtract_fusion.22
  103.2 2.0 add_reduce_fusion.16
  115.4 2.0 fusion.225
  117.4 1.9 convolution_add_fusion.20
  119.3 2.4 add_bitcast_fusion.5
  125.8 3.8 add.757
  129.7 114.4 %all-reduce.7.cloned.1.call-done = f32[4,2,256,256]{3,2,1,0:T(8,128)} async-done(((f32[4,2,256,256]{3,2,1,0:T(8,128)}), f32[4,2,256,256]{3,2,1,0:T(8,128)}) %all-reduce.7.cloned.1.call-update) | async-done | bytes 2097168 | tf_op jit(solution)/shard_map/psum | solution.py:109
  249.0 63.1 %psum.86 = f32[]{:T(128)} all-reduce(f32[]{:T(128)S(6)} %add.758), channel_id=1, replica_groups=mesh['wide'=32,'narrow'=4] {'wide'}, use_global_device_ids=true, to_apply=%region_14.15 | all-reduce | flops 1 | bytes 8 | tf_op jit(solution)/shard_map/psum | solution.py:109
  312.1 9.0 psum.87
  321.8 2.6 divide_subtract_fusion.3
  324.4 37.1 %conditional.8 = (f32[2,256,256]{2,1,0:T(8,128)}, f32[]{:T(128)}, f32[4,2,256,256]{3,2,1,0:T(8,128)}) conditional(s32[]{:T(128)} %bitcast.188, () %tuple.84, (f32[4,2,256,256]{3,2,1,0:T(8,128)S(1)}, f32[2,768,768]{2,1,0:T(8,128)}, s32[]{:T(128)}, s32[]{:T(128)}, f32[256,256]{1,0:T(8,128)S(1)}, /*index=5*/f32[256,256]{1,0:T(8,128)S(1)}, ...), branch_computations={%region_16.17_spmd, %region_17.22_spmd} | conditional | flops 12897091584 | bytes 71303224 | solution.py:102
  324.4 1.9 add_reduce_fusion.2
  337.6 2.0 convolution_subtract_fusion.2
  339.6 2.0 add_reduce_fusion.1
  351.8 2.0 fusion.20
  353.8 1.9 convolution_add_fusion
  355.7 2.4 add_bitcast_fusion
  361.5 11.8 %conditional.9 = (f32[2,256,256]{2,1,0:T(8,128)}, f32[]{:T(128)}, f32[4,2,256,256]{3,2,1,0:T(8,128)}) conditional(s32[]{:T(128)} %bitcast.193, () %tuple.86, (f32[4,2,256,256]{3,2,1,0:T(8,128)S(1)}, f32[2,768,768]{2,1,0:T(8,128)}, s32[]{:T(128)}, s32[]{:T(128)}, f32[256,256]{1,0:T(8,128)S(1)}, /*index=5*/f32[256,256]{1,0:T(8,128)S(1)}, ...), branch_computations={%region_22.23_spmd, %region_23.28_spmd} | conditional | flops 12897091584 | bytes 71303224 | solution.py:102
  373.4 3.8 add.777
  377.3 132.3 %all-reduce.11.cloned.1.call-done = f32[4,2,256,256]{3,2,1,0:T(8,128)} async-done(((f32[4,2,256,256]{3,2,1,0:T(8,128)}), f32[4,2,256,256]{3,2,1,0:T(8,128)}) %all-reduce.11.cloned.1.call-update) | async-done | bytes 2097168 | tf_op jit(solution)/shard_map/psum | solution.py:109
  514.6 2.5 broadcast_in_dim.2
  517.1 6.5 dynamic_update_slice.18
  525.1 63.1 %psum.90 = f32[]{:T(128)} all-reduce(f32[]{:T(128)S(6)} %add.778), channel_id=1, replica_groups=mesh['wide'=32,'narrow'=4] {'wide'}, use_global_device_ids=true, to_apply=%region_30.31 | all-reduce | flops 1 | bytes 8 | tf_op jit(solution)/shard_map/psum | solution.py:109
  588.3 6.6 dynamic_update_slice.19
  594.9 9.3 psum.91
  606.3 6.4 dynamic_update_slice.20
  614.3 6.6 dynamic_update_slice.21
  620.8 3.2 divide_subtract_fusion.2
  624.0 11.7 %conditional.10 = (f32[2,256,256]{2,1,0:T(8,128)}, f32[]{:T(128)}, f32[4,2,256,256]{3,2,1,0:T(8,128)}) conditional(s32[]{:T(128)} %bitcast.198, () %tuple.88, (f32[4,2,256,256]{3,2,1,0:T(8,128)}, f32[2,768,768]{2,1,0:T(8,128)}, s32[]{:T(128)}, s32[]{:T(128)}, f32[256,256]{1,0:T(8,128)S(1)}, /*index=5*/f32[256,256]{1,0:T(8,128)S(1)}, ...), branch_computations={%region_32.33_spmd, %region_33.38_spmd} | conditional | flops 12897091584 | bytes 79691856 | solution.py:102
  637.4 6.8 dynamic_update_slice.22
  644.2 4.8 conditional.11
  650.4 6.9 dynamic_update_slice.23
  658.4 66.7 %collective-permute-start.4 = (f32[2,768,128]{2,1,0:T(8,128)S(1)}, f32[2,768,128]{2,1,0:T(8,128)}, u32[]{:S(2)}, u32[]{:S(2)}) collective-permute-start(f32[2,768,128]{2,1,0:T(8,128)S(1)} %slice.336), channel_id=1, source_target_pairs={{4,0},{8,4},{12,8},{16,12},{20,16},{24,20},{28,24},{32,28},{36,32}... | collective-permute-start | bytes 2359304 | tf_op jit(solution)/shard_map/ppermute | solution.py:27
  725.1 3.8 add.793
  729.0 3.0 fusion.259
  732.1 1.9 collective-permute-start.5
  734.0 96.4 %all-reduce.15.cloned.1.call-done = f32[4,2,256,256]{3,2,1,0:T(8,128)} async-done(((f32[4,2,256,256]{3,2,1,0:T(8,128)}), f32[4,2,256,256]{3,2,1,0:T(8,128)}) %all-reduce.15.cloned.1.call-update) | async-done | bytes 2097168 | tf_op jit(solution)/shard_map/psum | solution.py:109
  830.5 2.2 fusion.248
  832.6 2.2 fusion.258
  836.2 4.0 collective-permute-start.7
  840.2 63.7 %psum.94 = f32[]{:T(128)} all-reduce(f32[]{:T(128)S(6)} %add.794), channel_id=1, replica_groups=mesh['wide'=32,'narrow'=4] {'wide'}, use_global_device_ids=true, to_apply=%region_46.47 | all-reduce | flops 1 | bytes 8 | tf_op jit(solution)/shard_map/psum | solution.py:109
  903.9 7.8 psum.95
  912.3 3.1 slice.339
  915.4 1.9 fusion.251
  917.3 1.9 fusion.250
  924.0 4.1 divide_subtract_fusion
  (101 shorter events, 97.6 us)
Async XLA Ops:
  7.2 12.6 %copy-start.3 = (f32[2,512,512]{2,1,0:T(8,128)S(1)}, f32[2,512,512]{2,1,0:T(8,128)}, u32[]{:S(2)}) copy-start(f32[2,512,512]{2,1,0:T(8,128)} %param.25) | copy-start | bytes 6291460
  7.2 236.9 %all-reduce.7.cloned.1.call-start = ((), (), s32[]{:S(2)}) async-start(), calls=%async_computation | async-start | bytes 4194304 | tf_op jit(solution)/shard_map/psum | solution.py:109
  8.6 11.0 %collective-permute-start = (f32[2,512,128]{2,1,0:T(8,128)S(1)}, f32[2,512,128]{2,1,0:T(8,128)S(1)}, u32[]{:S(2)}, u32[]{:S(2)}) collective-permute-start(f32[2,512,128]{2,1,0:T(8,128)S(1)} %get-tuple-element.871), channel_id=1, source_target_pairs={{0,4},{4,8},{8,12},{12,16},{16,20},{20,24},{24,28},{28,32},{32,36}... | collective-permute-start | bytes 1572872 | tf_op jit(solution)/shard_map/ppermute | solution.py:18
  13.6 10.5 %collective-permute-start.1 = (f32[2,512,128]{2,1,0:T(8,128)S(1)}, f32[2,512,128]{2,1,0:T(8,128)S(1)}, u32[]{:S(2)}, u32[]{:S(2)}) collective-permute-start(f32[2,512,128]{2,1,0:T(8,128)S(1)} %get-tuple-element.870), channel_id=1, source_target_pairs={{4,0},{8,4},{12,8},{16,12},{20,16},{24,20},{28,24},{32,28},{36,32}... | collective-permute-start | bytes 1572872 | tf_op jit(solution)/shard_map/ppermute | solution.py:19
  19.9 11.6 %copy-start.7 = (s32[1,1,6,2]{2,3,1,0:T(2,128)S(1)}, s32[1,1,6,2]{2,3,1,0:T(2,128)}, u32[]{:S(2)}) copy-start(s32[1,1,6,2]{2,3,1,0:T(2,128)} %param.28) | copy-start | bytes 148
  24.1 1.7 copy-start.5
  27.1 14.5 %collective-permute-start.2 = (f32[2,128,768]{2,1,0:T(8,128)}, f32[2,128,768]{2,1,0:T(8,128)S(1)}, u32[]{:S(2)}, u32[]{:S(2)}) collective-permute-start(f32[2,128,768]{2,1,0:T(8,128)} %get-tuple-element.868), channel_id=1, source_target_pairs={{0,1},{1,2},{2,3},{4,5},{5,6},{6,7},{8,9},{9,10},{10,11},{12,13},{... | collective-permute-start | bytes 2359304 | tf_op jit(solution)/shard_map/ppermute | solution.py:18
  30.2 15.5 %collective-permute-start.3 = (f32[2,128,768]{2,1,0:T(8,128)}, f32[2,128,768]{2,1,0:T(8,128)}, u32[]{:S(2)}, u32[]{:S(2)}) collective-permute-start(f32[2,128,768]{2,1,0:T(8,128)} %get-tuple-element.869), channel_id=1, source_target_pairs={{1,0},{2,1},{3,2},{5,4},{6,5},{7,6},{9,8},{10,9},{11,10},{13,12},{... | collective-permute-start | bytes 2359304 | tf_op jit(solution)/shard_map/ppermute | solution.py:19
  38.8 11.5 %copy-start.2 = (f32[4,2,256,256]{3,2,1,0:T(8,128)S(1)}, f32[4,2,256,256]{3,2,1,0:T(8,128)}, u32[]{:S(2)}) copy-start(f32[4,2,256,256]{3,2,1,0:T(8,128)} %param.26) | copy-start | bytes 6291460
  129.6 192.2 %all-reduce.9.cloned.1.call-start = ((), (), s32[]{:S(2)}) async-start(), calls=%async_computation.1 | async-start | bytes 4194304 | tf_op jit(solution)/shard_map/psum | solution.py:109
  244.1 265.5 %all-reduce.11.cloned.1.call-start = ((), (), s32[]{:S(2)}) async-start(), calls=%async_computation.2 | async-start | bytes 4194304 | tf_op jit(solution)/shard_map/psum | solution.py:109
  377.2 243.6 %all-reduce.13.cloned.1.call-start = ((), (), s32[]{:S(2)}) async-start(), calls=%async_computation.3 | async-start | bytes 4194304 | tf_op jit(solution)/shard_map/psum | solution.py:109
  509.6 320.8 %all-reduce.15.cloned.1.call-start = ((), (), s32[]{:S(2)}) async-start(), calls=%async_computation.4 | async-start | bytes 4194304 | tf_op jit(solution)/shard_map/psum | solution.py:109
  635.7 8.5 copy-start
  658.4 70.6 %collective-permute-start.4 = (f32[2,768,128]{2,1,0:T(8,128)S(1)}, f32[2,768,128]{2,1,0:T(8,128)}, u32[]{:S(2)}, u32[]{:S(2)}) collective-permute-start(f32[2,768,128]{2,1,0:T(8,128)S(1)} %slice.336), channel_id=1, source_target_pairs={{4,0},{8,4},{12,8},{16,12},{20,16},{24,20},{28,24},{32,28},{36,32}... | collective-permute-start | bytes 2359304 | tf_op jit(solution)/shard_map/ppermute | solution.py:27
  729.0 190.3 %all-reduce.17.cloned.1.call-start = ((), (), s32[]{:S(2)}) async-start(), calls=%async_computation.5 | async-start | bytes 4194304 | tf_op jit(solution)/shard_map/psum | solution.py:109
  732.1 98.4 %collective-permute-start.5 = (f32[2,768,128]{2,1,0:T(8,128)}, f32[2,768,128]{2,1,0:T(8,128)S(1)}, u32[]{:S(2)}, u32[]{:S(2)}) collective-permute-start(f32[2,768,128]{2,1,0:T(8,128)} %get-tuple-element.866), channel_id=1, source_target_pairs={{0,4},{4,8},{8,12},{12,16},{16,20},{20,24},{24,28},{28,32},{32,36}... | collective-permute-start | bytes 2359304 | tf_op jit(solution)/shard_map/ppermute | solution.py:27
  834.9 80.5 %collective-permute-start.6 = (f32[2,128,512]{2,1,0:T(8,128)}, f32[2,128,512]{2,1,0:T(8,128)S(1)}, u32[]{:S(2)}, u32[]{:S(2)}) collective-permute-start(f32[2,128,512]{2,1,0:T(8,128)} %get-tuple-element.865), channel_id=1, source_target_pairs={{1,0},{2,1},{3,2},{5,4},{6,5},{7,6},{9,8},{10,9},{11,10},{13,12},{... | collective-permute-start | bytes 1572872 | tf_op jit(solution)/shard_map/ppermute | solution.py:27
  836.2 81.2 %collective-permute-start.7 = (f32[2,128,512]{2,1,0:T(8,128)}, f32[2,128,512]{2,1,0:T(8,128)S(1)}, u32[]{:S(2)}, u32[]{:S(2)}) collective-permute-start(f32[2,128,512]{2,1,0:T(8,128)} %get-tuple-element.864), channel_id=1, source_target_pairs={{0,1},{1,2},{2,3},{4,5},{5,6},{6,7},{8,9},{9,10},{10,11},{12,13},{... | collective-permute-start | bytes 1572872 | tf_op jit(solution)/shard_map/ppermute | solution.py:27
  921.1 1.3 copy-start.6
  922.4 1.6 copy-start.4
Sparse Core Ops, SparseCore 0:
  129.7 114.2 all-reduce.6
  246.4 57.9 all-reduce.8
  377.3 132.2 all-reduce.10
  511.8 58.0 all-reduce.12
  729.1 101.2 all-reduce.14
  832.7 67.4 all-reduce.16
